TPU v7x, 16 devices: a whole 2x2x2 slice. The times are simulated.
16 devices in a mesh: dp: 4 (over z, y), tp: 4 (over x, core).
Axes of the slice: x: 2, y: 2, z: 2, core: 2. Of those that a mesh axis runs over, the one named last changes fastest.
Arguments:
- hidden: bfloat16 [64, 448, 2048], P('dp', 'tp'), parts along dimension 0
- prefix_len: int32 [64], P('dp'), parts along dimension 0
- valid_len: int32 [64], P('dp'), parts along dimension 0
- norm_attn: bfloat16 [2048], replicated
- w_query: bfloat16 [2048, 2048], P(None, 'tp')
- w_key: bfloat16 [2048, 256], replicated
- w_value: bfloat16 [2048, 256], replicated
- w_out: bfloat16 [2048, 2048], P('tp')
- norm_mlp: bfloat16 [2048], replicated
- w_gate: bfloat16 [2048, 16384], P(None, 'tp')
- w_up: bfloat16 [2048, 16384], P(None, 'tp')
- w_down: bfloat16 [16384, 2048], P('tp')
Outputs:
- output 1: bfloat16 [64, 448, 2048], P('dp', 'tp'), parts along dimension 0
- output 2: bfloat16 [64, 448, 256], P('dp', 'tp'), parts along dimension 0
- output 3: bfloat16 [64, 448, 256], P('dp', 'tp'), parts along dimension 0
There are 4 independent parts. A program takes and returns all parts, laid end to end along the dimension named above; an argument that names none is the same for every part.
All inputs are finite; a program needn't handle non-finite values.
Results may differ from a plain program's by a relative error of at most 0.0119926.
Values are sent between devices in bfloat16 or wider.
A program may use at most 1 GiB of HBM per device.

v0:
```python
import functools

import jax
import jax.numpy as jnp
from jax import lax
from jax.experimental import pallas as pl
from jax.experimental.pallas import tpu as pltpu
from jax.sharding import PartitionSpec as P


NORM_EPS = 1e-6
ROPE_BASE = 10000.0
MASK_FILL = -1e30
GELU_A = 0.7978845608028654
GELU_B = 0.7978845608028654 * 0.044715
MIB = 1024 * 1024

F_TILE = 512
ROW_BLOCK = 448

VMEM_MIB = 63


ANY = pl.BlockSpec(memory_space=pl.ANY)
SMEM = pl.BlockSpec(memory_space=pltpu.SMEM)


def params(limit_mib, **kw):
    return pltpu.CompilerParams(vmem_limit_bytes=limit_mib * MIB, **kw)


def cost(flops, nbytes):
    return pl.CostEstimate(flops=int(flops), bytes_accessed=int(nbytes), transcendentals=0)


def fdot(a, b):
    return jnp.dot(a, b, preferred_element_type=jnp.float32)


def rope_tables(positions, head_dim):
    half_dim = head_dim // 2
    inv_freq = ROPE_BASE ** (-2.0 * jnp.arange(half_dim, dtype=jnp.float32) / head_dim)
    angles = positions.astype(jnp.float32)[:, None] * inv_freq[None, :]
    return jnp.cos(angles), jnp.sin(angles)


def norm_rows(acts, gain):
    inv_rms = lax.rsqrt(jnp.mean(acts * acts, axis=-1, keepdims=True) + NORM_EPS)
    return (acts * inv_rms * gain).astype(jnp.bfloat16)


def rope_halves(vec, cos, sin):
    half = vec.shape[-1] // 2
    a, c = vec[..., :half], vec[..., half:]
    return a * cos - c * sin, c * cos + a * sin


def kv_kernel(h_ref, gain_ref, wk_ref, wv_ref, cos_ref, sin_ref, x_ref, k_ref, v_ref, kva_ref, kvb_ref):
    nb, rows, d = h_ref.shape
    gain = 1.0 + gain_ref[...].astype(jnp.float32)
    for b in range(nb):
        x_ref[b] = norm_rows(h_ref[b].astype(jnp.float32), gain)
    x = x_ref[...].reshape(nb * rows, d)
    key = fdot(x, wk_ref[...]).reshape(nb, rows, -1)
    lo, hi = rope_halves(key, cos_ref[...][None], sin_ref[...][None])
    half = lo.shape[-1]
    k_ref[:, :, :half] = lo.astype(jnp.bfloat16)
    k_ref[:, :, half:] = hi.astype(jnp.bfloat16)
    v_ref[...] = fdot(x, wv_ref[...]).astype(jnp.bfloat16).reshape(nb, rows, -1)
    first = pl.program_id(0) < pl.num_programs(0) // 2

    @pl.when(first)
    def _():
        kva_ref[:, :, :2 * half] = k_ref[...]
        kva_ref[:, :, 2 * half:] = v_ref[...]

    @pl.when(jnp.logical_not(first))
    def _():
        kvb_ref[:, :, :2 * half] = k_ref[...]
        kvb_ref[:, :, 2 * half:] = v_ref[...]


def kv_call(hidden, gain, w_key, w_value, cos, sin):
    nb, rows, d = hidden.shape
    hd = w_key.shape[1]
    step = ROW_BLOCK // rows
    steps = nb // step
    full = lambda *shape: pl.BlockSpec(shape, lambda i: (0,) * len(shape))
    blk = lambda w: pl.BlockSpec((step, rows, w), lambda i: (i, 0, 0))
    kva = pl.BlockSpec((step, rows, 2 * hd), lambda i: (jnp.minimum(i, steps // 2 - 1), 0, 0))
    kvb = pl.BlockSpec((step, rows, 2 * hd), lambda i: (jnp.maximum(i - steps // 2, 0), 0, 0))
    return pl.pallas_call(
        kv_kernel,
        grid=(steps,),
        in_specs=[blk(d), full(1, d), full(d, hd), full(d, hd), full(rows, hd // 2), full(rows, hd // 2)],
        out_specs=[blk(d), blk(hd), blk(hd), kva, kvb],
        out_shape=[jax.ShapeDtypeStruct((n, rows, w), jnp.bfloat16) for n, w in ((nb, d), (nb, hd), (nb, hd), (nb // 2, 2 * hd), (nb // 2, 2 * hd))],
        compiler_params=params(VMEM_MIB),
        cost_estimate=cost(4 * nb * rows * d * hd, 4 * nb * rows * d),
        name="kv_proj",
    )(hidden, gain, w_key, w_value, cos, sin)


def load_parts(parts, dst, sems, offsets):
    for i, (ref, off) in enumerate(zip(parts, offsets)):
        pltpu.make_async_copy(ref, dst.at[pl.ds(off, ref.shape[0])], sems.at[i]).start()
    for i, (ref, off) in enumerate(zip(parts, offsets)):
        pltpu.make_async_copy(ref, dst.at[pl.ds(off, ref.shape[0])], sems.at[i]).wait()


def query_body(head_dim, x_ref, weights, cos_ref, sin_ref, q_ref):
    nb, rows, d = x_ref.shape
    x = x_ref[...].reshape(nb * rows, d)
    cos, sin = cos_ref[...][None], sin_ref[...][None]
    scale = head_dim ** -0.5
    half = head_dim // 2
    for head in range(q_ref.shape[1]):
        vec = fdot(x, weights(head)).reshape(nb, rows, head_dim)
        lo, hi = rope_halves(vec, cos, sin)
        q_ref[:, head, :, :half] = (lo * scale).astype(jnp.bfloat16)
        q_ref[:, head, :, half:] = (hi * scale).astype(jnp.bfloat16)


def query_near_kernel(head_dim, x_ref, w0_ref, w1_ref, cos_ref, sin_ref, q_ref):
    per = w0_ref.shape[1] // head_dim

    def weights(head):
        ref = (w0_ref, w1_ref)[head // per]
        return ref[:, (head % per) * head_dim:(head % per + 1) * head_dim]

    query_body(head_dim, x_ref, weights, cos_ref, sin_ref, q_ref)


def query_far_kernel(head_dim, group_ref, x_ref, *rest):
    pieces, (cos_ref, sin_ref, q_ref, w_scr, sems) = rest[:8], rest[8:]
    size = pieces[0].shape[0]
    span = 4 * size

    @pl.when(pl.program_id(0) == 0)
    def _():
        offs = [pl.multiple_of(group_ref[k] * size, size) + s * span for s in range(2) for k in range(4)]
        load_parts(pieces, w_scr, sems, offs)

    per = w_scr.shape[1] // head_dim

    def weights(head):
        s = head // per
        return w_scr[s * span:(s + 1) * span, (head % per) * head_dim:(head % per + 1) * head_dim]

    query_body(head_dim, x_ref, weights, cos_ref, sin_ref, q_ref)


def query_call(x, weights, cos, sin, head_dim, group=None):
    nb, rows, d = x.shape
    width = weights[0].shape[1]
    heads = 2 * width // head_dim
    step = ROW_BLOCK // rows
    full = lambda *shape: pl.BlockSpec(shape, lambda i: (0,) * len(shape))
    x_spec = pl.BlockSpec((step, rows, d), lambda i: (i, 0, 0))
    tabs = [full(rows, head_dim // 2)] * 2
    if group is None:
        kernel, specs, args, scratch = query_near_kernel, [x_spec] + [full(d, width)] * 2 + tabs, (x, *weights, cos, sin), []
    else:
        kernel, specs, args = query_far_kernel, [SMEM, x_spec] + [ANY] * 8 + tabs, (group, x, *weights, cos, sin)
        scratch = [pltpu.VMEM((2 * d, width), jnp.bfloat16), pltpu.SemaphoreType.DMA((8,))]
    return pl.pallas_call(
        functools.partial(kernel, head_dim),
        grid=(nb // step,),
        in_specs=specs,
        out_specs=pl.BlockSpec((step, heads, rows, head_dim), lambda i: (i, 0, 0, 0)),
        out_shape=jax.ShapeDtypeStruct((nb, heads, rows, head_dim), jnp.bfloat16),
        scratch_shapes=scratch,
        compiler_params=params(VMEM_MIB),
        cost_estimate=cost(4 * nb * rows * d * width, 2 * nb * rows * d),
        name="query_near" if group is None else "query_far",
    )(*args)


def attn_kernel(base, pos_ref, pre_ref, val_ref, qa_ref, qb_ref, kv0, kv1, kv2, kv3, o_ref, k_scr, v_scr):
    _, heads, rows, hd = qa_ref.shape
    b = pl.program_id(0) + base
    for p, kv_ref in enumerate((kv0, kv1, kv2, kv3)):
        k_scr[p * rows:(p + 1) * rows] = kv_ref[0, :, :hd]
        v_scr[p * rows:(p + 1) * rows] = kv_ref[0, :, hd:]
    seq = 4 * rows
    col = lax.broadcasted_iota(jnp.int32, (rows, seq), 1)
    row = lax.broadcasted_iota(jnp.int32, (rows, seq), 0) + pos_ref[0]
    start = jnp.full((rows, seq), pos_ref[0], jnp.int32)
    for p in range(1, 4):
        start = jnp.where(col >= p * rows, pos_ref[p] - p * rows, start)
    col = col + start
    allowed = (col < val_ref[b]) & ((col < pre_ref[b]) | (col <= row))
    bias = jnp.where(allowed, 0.0, MASK_FILL).astype(jnp.float32)[None]
    keys, vals = k_scr[...], v_scr[...]
    head = 0
    for q_ref in (qa_ref, qb_ref):
        for g in range(0, heads, 2):
            q = q_ref[0, g:g + 2].reshape(2 * rows, hd)
            s = lax.dot_general(q, keys, (((1,), (1,)), ((), ())), preferred_element_type=jnp.float32)
            s = jnp.where(bias < 0.0, MASK_FILL, s.reshape(2, rows, seq))
            e = jnp.exp(s - jnp.max(s, axis=-1, keepdims=True))
            pr = (e * (1.0 / jnp.sum(e, axis=-1, keepdims=True))).astype(jnp.bfloat16)
            o = fdot(pr.reshape(2 * rows, seq), vals).astype(jnp.bfloat16)
            for i in range(2):
                o_ref[0, :, (head + i) * hd:(head + i + 1) * hd] = o[i * rows:(i + 1) * rows]
            head += 2


def attn_call(base, count, pos, prefix_len, valid_len, qa, qb, kvs):
    _, heads, rows, hd = qa.shape
    d = 2 * heads * hd
    q_spec = pl.BlockSpec((1, heads, rows, hd), lambda i: (i + base, 0, 0, 0))
    kv_spec = pl.BlockSpec((1, rows, 2 * hd), lambda i: (i, 0, 0))
    return pl.pallas_call(
        functools.partial(attn_kernel, base),
        grid=(count,),
        in_specs=[SMEM] * 3 + [q_spec] * 2 + [kv_spec] * 4,
        out_specs=pl.BlockSpec((1, rows, d), lambda i: (i, 0, 0)),
        out_shape=jax.ShapeDtypeStruct((count, rows, d), jnp.bfloat16),
        scratch_shapes=[pltpu.VMEM((4 * rows, hd), jnp.bfloat16)] * 2,
        compiler_params=params(VMEM_MIB),
        cost_estimate=cost(4 * count * 2 * heads * rows * 4 * rows * hd * 2, 8 * count * rows * d),
        name="attention",
    )(pos, prefix_len, valid_len, qa, qb, *kvs)


def out_kernel(group_ref, o_ref, h_ref, *rest):
    weights, gain_ref, mid_ref, x_ref, w_scr, sems = rest[:10], *rest[10:]
    nb, rows, d = o_ref.shape
    wide, size = weights[0].shape[0], weights[2].shape[0]

    @pl.when(pl.program_id(0) == 0)
    def _():
        offs = [0, wide] + [pl.multiple_of(group_ref[k] * size, size) + s * wide for s in (2, 3) for k in range(4)]
        load_parts(weights, w_scr, sems, offs)

    gain = 1.0 + gain_ref[...].astype(jnp.float32)
    pair = 2
    for b in range(0, nb, pair):
        total = fdot(o_ref[b:b + pair].reshape(pair * rows, d), w_scr[...])
        res = h_ref[b:b + pair].reshape(pair * rows, d).astype(jnp.float32)
        mid = (res + total.astype(jnp.bfloat16).astype(jnp.float32)).astype(jnp.bfloat16)
        mid_ref[b * rows:(b + pair) * rows] = mid
        x_ref[b * rows:(b + pair) * rows] = norm_rows(mid.astype(jnp.float32), gain)


def out_call(base, o, hidden, group, weights, gain):
    count, rows, d = o.shape
    step = ROW_BLOCK // rows
    off = base // step
    full = lambda *shape: pl.BlockSpec(shape, lambda i: (0,) * len(shape))
    res_spec = pl.BlockSpec((ROW_BLOCK, d), lambda i: (i, 0))
    return pl.pallas_call(
        out_kernel,
        grid=(count // step,),
        in_specs=[SMEM, pl.BlockSpec((step, rows, d), lambda i: (i, 0, 0)),
                  pl.BlockSpec((step, rows, d), lambda i: (i + off, 0, 0))]
        + [ANY] * 10 + [full(1, d)],
        out_specs=[res_spec, res_spec],
        out_shape=[jax.ShapeDtypeStruct((count * rows, d), jnp.bfloat16)] * 2,
        scratch_shapes=[pltpu.VMEM((d, d), jnp.bfloat16), pltpu.SemaphoreType.DMA((10,))],
        compiler_params=params(VMEM_MIB),
        cost_estimate=cost(2 * count * rows * d * d, 8 * count * rows * d),
        name="out_proj",
    )(group, o, hidden, *weights, gain)


def mlp_kernel(xa_hbm, xb_hbm, mid_a, mid_b, wg0, wu0, wd0, out_hbm, wg1, wu1, wd1, in_a, in_b, send_a, send_b, ret_a, ret_b,
               xbuf, own, acc, stage, mid, their, gb, ub, db, sems, sem_x, sem_in, sem_out, far_send, far_recv, row_send, row_recv):
    m, _ = xa_hbm.shape
    tiles = wg0.shape[1] // F_TILE
    steps = 8 * tiles
    starts = (0, tiles, 2 * tiles, 4 * tiles, 6 * tiles, 7 * tiles)
    me = lax.axis_index("tp")
    size = lax.axis_size("tp")
    chip = lax.rem(me + size // 2, size)
    core = me + 1 - 2 * lax.rem(me, 2)

    barrier = pltpu.get_barrier_semaphore()
    for peer in (chip, core):
        pl.semaphore_signal(barrier, inc=1, device_id={"tp": peer}, device_id_type=pl.DeviceIdType.MESH)
    pl.semaphore_wait(barrier, 2)

    def remote(src, dst, ssem, rsem, peer):
        return pltpu.make_async_remote_copy(src_ref=src, dst_ref=dst, send_sem=ssem, recv_sem=rsem,
                                            device_id={"tp": peer}, device_id_type=pl.DeviceIdType.MESH)

    rows = [remote(src, dst, row_send.at[i], row_recv.at[i], chip)
            for i, (src, dst) in enumerate(((xa_hbm, in_a), (xb_hbm, in_b), (send_a, ret_a), (send_b, ret_b)))]
    far = [remote(src, dst, far_send.at[i], far_recv.at[i], core)
           for i, (src, dst) in enumerate(((wg0, wg1), (wu0, wu1), (wd0, wd1)))]
    rows[0].start()
    for c in far:
        c.start()

    def tile_copies(ws, t, slot):
        wg, wu, wd = ws
        cols = pl.ds(pl.multiple_of(t * F_TILE, F_TILE), F_TILE)
        return (
            pltpu.make_async_copy(wg.at[:, cols], gb.at[slot], sems.at[slot, 0]),
            pltpu.make_async_copy(wu.at[:, cols], ub.at[slot], sems.at[slot, 1]),
            pltpu.make_async_copy(wd.at[cols, :], db.at[slot], sems.at[slot, 2]),
        )

    def between(j, lo, hi):
        return (j >= lo * tiles) & (j < hi * tiles)

    def start(j, slot):
        use_far = between(j, 3, 4) | between(j, 5, 8)
        t = lax.rem(j, tiles)

        @pl.when(jnp.logical_not(use_far))
        def _():
            for c in tile_copies((wg0, wu0, wd0), t, slot):
                c.start()

        @pl.when(use_far)
        def _():
            for c in tile_copies((wg1, wu1, wd1), t, slot):
                c.start()

    def x_copy(src, slot):
        return pltpu.make_async_copy(src, xbuf.at[slot], sem_x.at[slot])

    x_copy(xa_hbm, 0).start()
    start(jnp.int32(0), 0)
    acc[...] = jnp.zeros_like(acc)
    x_sources = (xa_hbm, xb_hbm, in_a, in_b, xa_hbm, xb_hbm)
    chunk = ROW_BLOCK // 2

    def chunks(fn):
        @pl.loop(0, m // chunk)
        def _(i):
            fn(pl.ds(pl.multiple_of(i * chunk, chunk), chunk))

    def body(j, carry):
        slot = lax.rem(j, 2)

        @pl.when(j == 2 * tiles - 4)
        def _():
            rows[1].start()

        @pl.when(j == 3 * tiles - 2)
        def _():
            for c in far:
                c.wait_recv()

        for k in range(1, 6):
            @pl.when(j == starts[k] - 2)
            def _():
                if k in (2, 3):
                    rows[k - 2].wait_recv()
                x_copy(x_sources[k], k % 2).start()

        for k in (4, 5):
            @pl.when(j == starts[k] + tiles - 3)
            def _():
                pltpu.make_async_copy((mid_a, mid_b)[k - 4], mid, sem_in.at[0]).start()

        for k in (2, 3):
            @pl.when(j == starts[k + 1] + 1)
            def _():
                pltpu.make_async_copy(stage, (send_a, send_b)[k - 2], sem_out.at[0]).wait()
                rows[k].start()

        for k in range(6):
            @pl.when(j == starts[k])
            def _():
                x_copy(x_sources[k], k % 2).wait()

        @pl.when(j + 1 < steps)
        def _():
            start(j + 1, 1 - slot)

        for c in tile_copies((wg0, wu0, wd0), 0, slot):
            c.wait()

        first = j == starts[0]
        odd = jnp.int32(0)
        for k in range(1, 6):
            first = first | (j == starts[k])
            odd = odd + (j >= starts[k]).astype(jnp.int32)
        odd = lax.rem(odd, 2)
        acts = []
        for r in range(0, m, ROW_BLOCK):
            x = xbuf[odd, r:r + ROW_BLOCK]
            g = fdot(x, gb[slot])
            u = fdot(x, ub[slot])
            t = jnp.tanh(g * (GELU_A + GELU_B * (g * g)))
            acts.append((g * (0.5 + 0.5 * t) * u).astype(jnp.bfloat16))
        for i, r in enumerate(range(0, m, ROW_BLOCK)):
            acc[r:r + ROW_BLOCK] = jnp.where(first, 0.0, acc[r:r + ROW_BLOCK]) + fdot(acts[i], db[slot])

        for k in (0, 1):
            @pl.when(j == starts[k + 1] - 1)
            def _():
                def keep(sl):
                    own[k, sl] = acc[sl].astype(jnp.bfloat16)

                chunks(keep)

        for k in (2, 3):
            @pl.when(j == starts[k + 1] - 1)
            def _():
                def put(sl):
                    stage[sl] = acc[sl].astype(jnp.bfloat16)

                chunks(put)
                pltpu.make_async_copy(stage, (send_a, send_b)[k - 2], sem_out.at[0]).start()

        for k in (4, 5):
            @pl.when(j == starts[k] + tiles - 1)
            def _():
                ret, mid_hbm = ((ret_a, mid_a), (ret_b, mid_b))[k - 4]
                rows[k - 2].wait_recv()
                got = pltpu.make_async_copy(ret, their, sem_in.at[1])
                got.start()
                pltpu.make_async_copy(mid_hbm, mid, sem_in.at[0]).wait()
                got.wait()
                if k == 5:
                    pltpu.make_async_copy(stage, out_hbm.at[pl.ds(0, m)], sem_out.at[1]).wait()

                def finish(sl):
                    total = acc[sl] + own[k - 4, sl].astype(jnp.float32) + their[sl].astype(jnp.float32)
                    stage[sl] = (mid[sl].astype(jnp.float32) + total.astype(jnp.bfloat16).astype(jnp.float32)).astype(jnp.bfloat16)

                chunks(finish)
                pltpu.make_async_copy(stage, out_hbm.at[pl.ds((k - 4) * m, m)], sem_out.at[k - 3]).start()
        return carry

    lax.fori_loop(0, steps, body, 0)
    pltpu.make_async_copy(stage, out_hbm.at[pl.ds(m, m)], sem_out.at[2]).wait()
    for c in rows + far:
        c.wait_send()


def mlp_call(x_a, x_b, mid_a, mid_b, weights):
    m, d = x_a.shape
    f = weights[0].shape[1]
    half = jax.ShapeDtypeStruct((m, d), jnp.bfloat16)
    outs = [jax.ShapeDtypeStruct((2 * m, d), jnp.bfloat16)] + [jax.ShapeDtypeStruct(w.shape, w.dtype) for w in weights] + [half] * 6
    dma = pltpu.SemaphoreType.DMA
    return pl.pallas_call(
        mlp_kernel,
        in_specs=[ANY] * 7,
        out_specs=[ANY] * len(outs),
        out_shape=outs,
        scratch_shapes=[
            pltpu.VMEM((2, m, d), jnp.bfloat16), pltpu.VMEM((2, m, d), jnp.bfloat16), pltpu.VMEM((m, d), jnp.float32),
            pltpu.VMEM((m, d), jnp.bfloat16), pltpu.VMEM((m, d), jnp.bfloat16), pltpu.VMEM((m, d), jnp.bfloat16),
            pltpu.VMEM((2, d, F_TILE), jnp.bfloat16), pltpu.VMEM((2, d, F_TILE), jnp.bfloat16), pltpu.VMEM((2, F_TILE, d), jnp.bfloat16),
            dma((2, 3)), dma((2,)), dma((2,)), dma((3,)), dma((3,)), dma((3,)), dma((4,)), dma((4,)),
        ],
        compiler_params=params(60, collective_id=0, has_side_effects=True),
        cost_estimate=cost(48 * m * d * f, 48 * d * f),
        name="mlp",
    )(x_a, x_b, mid_a, mid_b, *weights)[0]


def solution(mesh):
    tp_size, dp_size = mesh.shape["tp"], mesh.shape["dp"]
    row_spec = P("dp", "tp", None)
    arg_specs = (row_spec, P("dp"), P("dp"), P(), P(None, "tp"), P(), P(), P("tp", None), P(), P(None, "tp"), P(None, "tp"), P("tp", None))

    def swap(a, axis, bit):
        return lax.ppermute(a, axis, [(i, i ^ bit) for i in range(mesh.shape[axis])])

    def spread(w, me_dp):
        size = w.shape[0] // dp_size
        quarter = lax.dynamic_slice_in_dim(w, me_dp * size, size, axis=0)
        return swap(quarter, "tp", 2)

    def gather(got, diag_first):
        y = swap(got, "dp", 1)
        z = swap(got, "dp", 2)
        diag = swap(y, "dp", 2) if diag_first else swap(z, "dp", 1)
        far = [got, y, z, diag]
        return far + [swap(a, "tp", 1) for a in far]

    def local_layer(hidden, prefix_len, valid_len, norm_attn, w_query, w_key, w_value, w_out, norm_mlp, w_gate, w_up, w_down):
        nb, rows, d = hidden.shape
        head_dim = w_key.shape[1]
        half = nb // 2
        me, me_dp = lax.axis_index("tp"), lax.axis_index("dp")
        group = jnp.bitwise_xor(me_dp, jnp.arange(dp_size, dtype=jnp.int32))
        pos = jnp.bitwise_xor(me, jnp.arange(tp_size, dtype=jnp.int32)) * rows
        cos, sin = rope_tables(me * rows + jnp.arange(rows), head_dim)

        wq_got = spread(w_query, me_dp)
        wo_got = spread(w_out, me_dp)
        w_query_c = swap(w_query, "tp", 1)
        normed, key_local, value_local, kv_a, kv_b = kv_call(hidden, norm_attn[None], w_key, w_value, cos, sin)
        kvs = []
        for kv in (kv_a, kv_b):
            kv_x = swap(kv, "tp", 2)
            kvs.append((kv, swap(kv, "tp", 1), kv_x, swap(kv_x, "tp", 1)))
        query_a = query_call(normed, (w_query, w_query_c), cos, sin, head_dim)
        query_b = query_call(normed, gather(wq_got, True), cos, sin, head_dim, group)
        w_outs = [w_out, swap(w_out, "tp", 1)] + gather(wo_got, False)
        near = (w_gate, w_up, w_down)

        mids, mine = [], []
        for base, kv in ((0, kvs[0]), (half, kvs[1])):
            o = attn_call(base, half, pos, prefix_len, valid_len, query_a, query_b, kv)
            mid, x = out_call(base, o, hidden, group, w_outs, norm_mlp[None])
            mids.append(mid)
            mine.append(x)
        out = mlp_call(*mine, *mids, near)
        return out.reshape(nb, rows, d), key_local, value_local

    return jax.shard_map(local_layer, mesh=mesh, in_specs=arg_specs, out_specs=(row_spec, row_spec, row_spec), check_vma=False)
```

profile of v0, /device:TPU:0, one launch (start us, length us, event | category | flops | bytes accessed | tf_op | source)
XLA Modules:
  0.0 599.3 jit_solution(13602192182634769753)
XLA Ops:
  0.6 1.1 constant_dynamic-slice_fusion
  1.7 3.2 collective-permute-start.13
  5.0 1.9 constant_dynamic-slice_fusion.1
  6.9 1.3 broadcast_in_dim.4.gain_ref
  9.2 11.1 %kv_proj.1 = (bf16[16,112,2048]{2,1,0:T(8,128)(2,1)}, bf16[16,112,256]{2,1,0:T(8,128)(2,1)}, bf16[16,112,256]{2,1,0:T(8,128)(2,1)}, bf16[8,112,512]{2,1,0:T(8,128)(2,1)}, bf16[8,112,512]{2,1,0:T(8,128)(2,1)}) custom-call(bf16[16,112,2048]{2,1,0:T(8,128)(2,1)} %h_ref.5, bf16[1,2048]{1,0:T(2,128)(2,1)} %broadcast_in_dim.4.gain_ref, bf16[2048,256]{1,0:T(8,128)(2,1)} %wk_ref.1, ...), custom_call_target="tpu_custom_call" | custom-call | flops 3758096384 | bytes 14680064 | tf_op jit(solution)/shard_map/kv_proj/pallas_call | solution.py:92
  20.2 2.0 collective-permute-start.10
  22.3 6.8 %collective-permute-done.1.rest_0_ = bf16[512,512]{1,0:T(8,128)(2,1)} collective-permute-done((bf16[512,512]{1,0:T(8,128)(2,1)}, bf16[512,512]{1,0:T(8,128)(2,1)}, u32[]{:S(2)}, u32[]{:S(2)}) %collective-permute-start.1) | collective-permute-done | bytes 524320 | tf_op jit(solution)/shard_map/ppermute | solution.py:466
  29.1 2.0 collective-permute-start.2
  31.1 17.6 %collective-permute-done.10.kv2 = bf16[8,112,512]{2,1,0:T(8,128)(2,1)} collective-permute-done((bf16[8,112,512]{2,1,0:T(8,128)(2,1)}, bf16[8,112,512]{2,1,0:T(8,128)(2,1)}, u32[]{:S(2)}, u32[]{:S(2)}) %collective-permute-start.10) | collective-permute-done | bytes 917536 | tf_op jit(solution)/shard_map/ppermute | solution.py:466
  48.7 18.8 %collective-permute-done.22.kv2 = bf16[8,112,512]{2,1,0:T(8,128)(2,1)} collective-permute-done((bf16[8,112,512]{2,1,0:T(8,128)(2,1)}, bf16[8,112,512]{2,1,0:T(8,128)(2,1)}, u32[]{:S(2)}, u32[]{:S(2)}) %collective-permute-start.22) | collective-permute-done | bytes 917536 | tf_op jit(solution)/shard_map/ppermute | solution.py:466
  67.5 1.8 collective-permute-start.3
  71.9 10.8 %collective-permute-done.3.rest_2_ = bf16[512,512]{1,0:T(8,128)(2,1)} collective-permute-done((bf16[512,512]{1,0:T(8,128)(2,1)}, bf16[512,512]{1,0:T(8,128)(2,1)}, u32[]{:S(2)}, u32[]{:S(2)}) %collective-permute-start.3) | collective-permute-done | bytes 524320 | tf_op jit(solution)/shard_map/ppermute | solution.py:466
  82.7 9.5 %collective-permute-done.4.rest_3_ = bf16[512,512]{1,0:T(8,128)(2,1)} collective-permute-done((bf16[512,512]{1,0:T(8,128)(2,1)}, bf16[512,512]{1,0:T(8,128)(2,1)}, u32[]{:S(2)}, u32[]{:S(2)}) %collective-permute-start.4) | collective-permute-done | bytes 524320 | tf_op jit(solution)/shard_map/ppermute | solution.py:466
  92.7 12.3 %query_near.1.qa_ref = bf16[16,4,112,256]{3,2,1,0:T(8,128)(2,1)} custom-call(bf16[16,112,2048]{2,1,0:T(8,128)(2,1)} %get-tuple-element.13.x_ref, bf16[2048,512]{1,0:T(8,128)(2,1)} %w0_ref.1, bf16[2048,512]{1,0:T(8,128)(2,1)} %collective-permute-done.w1_ref, f32[112,128]{1,0:T(8,128)} %get-tuple-element.24.cos_ref.rest_8_, ...), custom_call_target="tpu_custom_call" | custom-call | flops 7516192768 | bytes 7340032 | tf_op jit(solution)/shard_map/query_near/pallas_call | solution.py:166
  105.1 1.6 collective-permute-start.15
  106.9 13.4 %query_far.1.qb_ref = bf16[16,4,112,256]{3,2,1,0:T(8,128)(2,1)} custom-call(s32[4]{0:T(128)} %iota_xor_fusion.group_ref, bf16[16,112,2048]{2,1,0:T(8,128)(2,1)} %get-tuple-element.13.x_ref, bf16[512,512]{1,0:T(8,128)(2,1)} %collective-permute-done.1.rest_0_, bf16[512,512]{1,0:T(8,128)(2,1)} %collective-permute-done.2.rest_1_, ...), custom_call_target="tpu_custom_call" | custom-call | flops 7516192768 | bytes 7340032 | tf_op jit(solution)/shard_map/query_far/pallas_call | solution.py:166
  120.3 1.6 collective-permute-start.14
  122.4 12.8 %attention.3.o_ref = bf16[8,112,2048]{2,1,0:T(8,128)(2,1)} custom-call(s32[4]{0:T(128)} %xor_multiply_fusion.pos_ref, s32[16]{0:T(128)} %pre_ref.3, s32[16]{0:T(128)} %val_ref.3, bf16[16,4,112,256]{3,2,1,0:T(8,128)(2,1)} %query_near.1.qa_ref, bf16[16,4,112,256]{3,2,1,0:T(8,128)(2,1)} %query_far.1.qb_ref, bf16[8,112,512]{2,1,0:T(8,128)(2,1)} %get-tuple-element.16.kv0, ...), custom_call_target="tpu_custom_call" | custom-call | flops 6576668672 | bytes 14680064 | tf_op jit(solution)/shard_map/attention/pallas_call | solution.py:214
  135.7 10.4 %collective-permute-done.16.rest_5_ = bf16[128,2048]{1,0:T(8,128)(2,1)} collective-permute-done((bf16[128,2048]{1,0:T(8,128)(2,1)}, bf16[128,2048]{1,0:T(8,128)(2,1)}, u32[]{:S(2)}, u32[]{:S(2)}) %collective-permute-start.16) | collective-permute-done | bytes 524320 | tf_op jit(solution)/shard_map/ppermute | solution.py:466
  146.6 12.7 %attention.2.o_ref = bf16[8,112,2048]{2,1,0:T(8,128)(2,1)} custom-call(s32[4]{0:T(128)} %xor_multiply_fusion.pos_ref, s32[16]{0:T(128)} %pre_ref.3, s32[16]{0:T(128)} %val_ref.3, bf16[16,4,112,256]{3,2,1,0:T(8,128)(2,1)} %query_near.1.qa_ref, bf16[16,4,112,256]{3,2,1,0:T(8,128)(2,1)} %query_far.1.qb_ref, bf16[8,112,512]{2,1,0:T(8,128)(2,1)} %get-tuple-element.14.kv0, ...), custom_call_target="tpu_custom_call" | custom-call | flops 6576668672 | bytes 14680064 | tf_op jit(solution)/shard_map/attention/pallas_call | solution.py:214
  160.1 16.6 %out_proj.2 = (bf16[896,2048]{1,0:T(8,128)(2,1)}, bf16[896,2048]{1,0:T(8,128)(2,1)}) custom-call(s32[4]{0:T(128)} %iota_xor_fusion.group_ref, bf16[8,112,2048]{2,1,0:T(8,128)(2,1)} %attention.2.o_ref, bf16[16,112,2048]{2,1,0:T(8,128)(2,1)} %h_ref.5, bf16[512,2048]{1,0:T(8,128)(2,1)} %rest_0_.3, bf16[512,2048]{1,0:T(8,128)(2,1)} %collective-permute-done.12.rest_1_, ...), custom_call_target="tpu_custom_call" | custom-call | flops 7516192768 | bytes 14680064 | tf_op jit(solution)/shard_map/out_proj/pallas_call | solution.py:253
  176.7 16.8 %out_proj.3 = (bf16[896,2048]{1,0:T(8,128)(2,1)}, bf16[896,2048]{1,0:T(8,128)(2,1)}) custom-call(s32[4]{0:T(128)} %iota_xor_fusion.group_ref, bf16[8,112,2048]{2,1,0:T(8,128)(2,1)} %attention.3.o_ref, bf16[16,112,2048]{2,1,0:T(8,128)(2,1)} %h_ref.5, bf16[512,2048]{1,0:T(8,128)(2,1)} %rest_0_.3, bf16[512,2048]{1,0:T(8,128)(2,1)} %collective-permute-done.12.rest_1_, ...), custom_call_target="tpu_custom_call" | custom-call | flops 7516192768 | bytes 14680064 | tf_op jit(solution)/shard_map/out_proj/pallas_call | solution.py:253
  193.4 398.3 %mlp.1 = (bf16[1792,2048]{1,0:T(8,128)(2,1)}, bf16[2048,4096]{1,0:T(8,128)(2,1)}, bf16[2048,4096]{1,0:T(8,128)(2,1)}, bf16[4096,2048]{1,0:T(8,128)(2,1)}, bf16[8...) custom-call(bf16[896,2048]{1,0:T(8,128)(2,1)} %get-tuple-element.15., ...), custom_call_target="tpu_custom_call" | custom-call | flops 360777252864 | bytes 402653184 | tf_op jit(solution)/shard_map/mlp/pallas_call | solution.py:443
  591.7 7.5 %copy.16 = bf16[16,112,2048]{2,1,0:T(8,128)(2,1)} copy(bf16[16,112,2048]{2,1,0:T(8,128)(2,1)} %bitcast.1) | data formatting | bytes 14680064
  (52 shorter events, 6.7 us)
Async XLA Ops:
  1.7 29.4 %collective-permute-start.13 = (bf16[128,2048]{1,0:T(8,128)(2,1)S(1)}, bf16[128,2048]{1,0:T(8,128)(2,1)}, u32[]{:S(2)}, u32[]{:S(2)}) collective-permute-start(bf16[128,2048]{1,0:T(8,128)(2,1)S(1)} %constant_dynamic-slice_fusion), channel_id=1, source_target_pairs={{0,2},{1,3},{2,0},{3,1},{4,6},{5,7},{6,4},{7,5},{8,10},{9,11},{10,... | collective-permute-start | bytes 1572872 | tf_op jit(solution)/shard_map/ppermute | solution.py:466
  5.0 87.2 %collective-permute-start = (bf16[2048,512]{1,0:T(8,128)(2,1)}, bf16[2048,512]{1,0:T(8,128)(2,1)}, u32[]{:S(2)}, u32[]{:S(2)}) collective-permute-start(bf16[2048,512]{1,0:T(8,128)(2,1)} %w0_ref.1), channel_id=1, source_target_pairs={{0,1},{1,0},{2,3},{3,2},{4,5},{5,4},{6,7},{7,6},{8,9},{9,8},{10,11... | collective-permute-start | bytes 6291464 | tf_op jit(solution)/shard_map/ppermute | solution.py:466
  6.8 22.2 %collective-permute-start.1 = (bf16[512,512]{1,0:T(8,128)(2,1)}, bf16[512,512]{1,0:T(8,128)(2,1)}, u32[]{:S(2)}, u32[]{:S(2)}) collective-permute-start(bf16[512,512]{1,0:T(8,128)(2,1)} %constant_dynamic-slice_fusion.1), channel_id=1, source_target_pairs={{0,2},{1,3},{2,0},{3,1},{4,6},{5,7},{6,4},{7,5},{8,10},{9,11},{10,... | collective-permute-start | bytes 1572872 | tf_op jit(solution)/shard_map/ppermute | solution.py:466
  20.2 28.5 %collective-permute-start.10 = (bf16[8,112,512]{2,1,0:T(8,128)(2,1)}, bf16[8,112,512]{2,1,0:T(8,128)(2,1)}, u32[]{:S(2)}, u32[]{:S(2)}) collective-permute-start(bf16[8,112,512]{2,1,0:T(8,128)(2,1)} %get-tuple-element.14.kv0), channel_id=1, source_target_pairs={{0,2},{1,3},{2,0},{3,1},{4,6},{5,7},{6,4},{7,5},{8,10},{9,11},{10,... | collective-permute-start | bytes 2752520 | tf_op jit(solution)/shard_map/ppermute | solution.py:466
  22.2 45.4 %collective-permute-start.22 = (bf16[8,112,512]{2,1,0:T(8,128)(2,1)}, bf16[8,112,512]{2,1,0:T(8,128)(2,1)}, u32[]{:S(2)}, u32[]{:S(2)}) collective-permute-start(bf16[8,112,512]{2,1,0:T(8,128)(2,1)} %get-tuple-element.16.kv0), channel_id=1, source_target_pairs={{0,2},{1,3},{2,0},{3,1},{4,6},{5,7},{6,4},{7,5},{8,10},{9,11},{10,... | collective-permute-start | bytes 2752520 | tf_op jit(solution)/shard_map/ppermute | solution.py:466
  29.1 40.3 %collective-permute-start.2 = (bf16[512,512]{1,0:T(8,128)(2,1)}, bf16[512,512]{1,0:T(8,128)(2,1)}, u32[]{:S(2)}, u32[]{:S(2)}) collective-permute-start(bf16[512,512]{1,0:T(8,128)(2,1)} %collective-permute-done.1.rest_0_), channel_id=1, source_target_pairs={{0,4},{4,0},{8,12},{12,8},{1,5},{5,1},{9,13},{13,9},{2,6},{6,2},{1... | collective-permute-start | bytes 1572872 | tf_op jit(solution)/shard_map/ppermute | solution.py:466
  31.1 40.2 %collective-permute-start.21 = (bf16[8,112,512]{2,1,0:T(8,128)(2,1)}, bf16[8,112,512]{2,1,0:T(8,128)(2,1)S(1)}, u32[]{:S(2)}, u32[]{:S(2)}) collective-permute-start(bf16[8,112,512]{2,1,0:T(8,128)(2,1)} %get-tuple-element.16.kv0), channel_id=1, source_target_pairs={{0,1},{1,0},{2,3},{3,2},{4,5},{5,4},{6,7},{7,6},{8,9},{9,8},{10,11... | collective-permute-start | bytes 2752520 | tf_op jit(solution)/shard_map/ppermute | solution.py:466
  48.7 22.6 %collective-permute-start.5 = (bf16[512,512]{1,0:T(8,128)(2,1)}, bf16[512,512]{1,0:T(8,128)(2,1)S(1)}, u32[]{:S(2)}, u32[]{:S(2)}) collective-permute-start(bf16[512,512]{1,0:T(8,128)(2,1)} %collective-permute-done.1.rest_0_), channel_id=1, source_target_pairs={{0,1},{1,0},{2,3},{3,2},{4,5},{5,4},{6,7},{7,6},{8,9},{9,8},{10,11... | collective-permute-start | bytes 1572872 | tf_op jit(solution)/shard_map/ppermute | solution.py:466
  67.5 15.1 %collective-permute-start.3 = (bf16[512,512]{1,0:T(8,128)(2,1)}, bf16[512,512]{1,0:T(8,128)(2,1)}, u32[]{:S(2)}, u32[]{:S(2)}) collective-permute-start(bf16[512,512]{1,0:T(8,128)(2,1)} %collective-permute-done.1.rest_0_), channel_id=1, source_target_pairs={{0,8},{4,12},{8,0},{12,4},{1,9},{5,13},{9,1},{13,5},{2,10},{6,14},... | collective-permute-start | bytes 1572872 | tf_op jit(solution)/shard_map/ppermute | solution.py:466
  69.4 22.8 %collective-permute-start.4 = (bf16[512,512]{1,0:T(8,128)(2,1)}, bf16[512,512]{1,0:T(8,128)(2,1)}, u32[]{:S(2)}, u32[]{:S(2)}) collective-permute-start(bf16[512,512]{1,0:T(8,128)(2,1)} %collective-permute-done.2.rest_1_), channel_id=1, source_target_pairs={{0,8},{4,12},{8,0},{12,4},{1,9},{5,13},{9,1},{13,5},{2,10},{6,14},... | collective-permute-start | bytes 1572872 | tf_op jit(solution)/shard_map/ppermute | solution.py:466
  71.4 88.0 %collective-permute-start.12 = (bf16[512,2048]{1,0:T(8,128)(2,1)}, bf16[512,2048]{1,0:T(8,128)(2,1)}, u32[]{:S(2)}, u32[]{:S(2)}) collective-permute-start(bf16[512,2048]{1,0:T(8,128)(2,1)} %rest_0_.3), channel_id=1, source_target_pairs={{0,1},{1,0},{2,3},{3,2},{4,5},{5,4},{6,7},{7,6},{8,9},{9,8},{10,11... | collective-permute-start | bytes 6291464 | tf_op jit(solution)/shard_map/ppermute | solution.py:466
  71.4 50.5 %collective-permute-start.23 = (bf16[8,112,512]{2,1,0:T(8,128)(2,1)}, bf16[8,112,512]{2,1,0:T(8,128)(2,1)}, u32[]{:S(2)}, u32[]{:S(2)}) collective-permute-start(bf16[8,112,512]{2,1,0:T(8,128)(2,1)} %collective-permute-done.22.kv2), channel_id=1, source_target_pairs={{0,1},{1,0},{2,3},{3,2},{4,5},{5,4},{6,7},{7,6},{8,9},{9,8},{10,11... | collective-permute-start | bytes 2752520 | tf_op jit(solution)/shard_map/ppermute | solution.py:466
  82.7 22.5 %collective-permute-start.6 = (bf16[512,512]{1,0:T(8,128)(2,1)}, bf16[512,512]{1,0:T(8,128)(2,1)}, u32[]{:S(2)}, u32[]{:S(2)}) collective-permute-start(bf16[512,512]{1,0:T(8,128)(2,1)} %collective-permute-done.2.rest_1_), channel_id=1, source_target_pairs={{0,1},{1,0},{2,3},{3,2},{4,5},{5,4},{6,7},{7,6},{8,9},{9,8},{10,11... | collective-permute-start | bytes 1572872 | tf_op jit(solution)/shard_map/ppermute | solution.py:466
  92.2 12.9 %collective-permute-start.7 = (bf16[512,512]{1,0:T(8,128)(2,1)}, bf16[512,512]{1,0:T(8,128)(2,1)}, u32[]{:S(2)}, u32[]{:S(2)}) collective-permute-start(bf16[512,512]{1,0:T(8,128)(2,1)} %collective-permute-done.3.rest_2_), channel_id=1, source_target_pairs={{0,1},{1,0},{2,3},{3,2},{4,5},{5,4},{6,7},{7,6},{8,9},{9,8},{10,11... | collective-permute-start | bytes 1572872 | tf_op jit(solution)/shard_map/ppermute | solution.py:466
  92.2 14.5 %collective-permute-start.8 = (bf16[512,512]{1,0:T(8,128)(2,1)}, bf16[512,512]{1,0:T(8,128)(2,1)}, u32[]{:S(2)}, u32[]{:S(2)}) collective-permute-start(bf16[512,512]{1,0:T(8,128)(2,1)} %collective-permute-done.4.rest_3_), channel_id=1, source_target_pairs={{0,1},{1,0},{2,3},{3,2},{4,5},{5,4},{6,7},{7,6},{8,9},{9,8},{10,11... | collective-permute-start | bytes 1572872 | tf_op jit(solution)/shard_map/ppermute | solution.py:466
  105.1 30.1 %collective-permute-start.9 = (bf16[8,112,512]{2,1,0:T(8,128)(2,1)S(1)}, bf16[8,112,512]{2,1,0:T(8,128)(2,1)}, u32[]{:S(2)}, u32[]{:S(2)}) collective-permute-start(bf16[8,112,512]{2,1,0:T(8,128)(2,1)S(1)} %copy-done.1), channel_id=1, source_target_pairs={{0,1},{1,0},{2,3},{3,2},{4,5},{5,4},{6,7},{7,6},{8,9},{9,8},{10,11... | collective-permute-start | bytes 2752520 | tf_op jit(solution)/shard_map/ppermute | solution.py:466
  105.1 15.2 %collective-permute-start.15 = (bf16[128,2048]{1,0:T(8,128)(2,1)}, bf16[128,2048]{1,0:T(8,128)(2,1)}, u32[]{:S(2)}, u32[]{:S(2)}) collective-permute-start(bf16[128,2048]{1,0:T(8,128)(2,1)} %collective-permute-done.13.rest_2_), channel_id=1, source_target_pairs={{0,8},{4,12},{8,0},{12,4},{1,9},{5,13},{9,1},{13,5},{2,10},{6,14},... | collective-permute-start | bytes 1572872 | tf_op jit(solution)/shard_map/ppermute | solution.py:466
  106.7 39.4 %collective-permute-start.11 = (bf16[8,112,512]{2,1,0:T(8,128)(2,1)}, bf16[8,112,512]{2,1,0:T(8,128)(2,1)}, u32[]{:S(2)}, u32[]{:S(2)}) collective-permute-start(bf16[8,112,512]{2,1,0:T(8,128)(2,1)} %collective-permute-done.10.kv2), channel_id=1, source_target_pairs={{0,1},{1,0},{2,3},{3,2},{4,5},{5,4},{6,7},{7,6},{8,9},{9,8},{10,11... | collective-permute-start | bytes 2752520 | tf_op jit(solution)/shard_map/ppermute | solution.py:466
  120.3 15.1 %collective-permute-start.14 = (bf16[128,2048]{1,0:T(8,128)(2,1)}, bf16[128,2048]{1,0:T(8,128)(2,1)}, u32[]{:S(2)}, u32[]{:S(2)}) collective-permute-start(bf16[128,2048]{1,0:T(8,128)(2,1)} %collective-permute-done.13.rest_2_), channel_id=1, source_target_pairs={{0,4},{4,0},{8,12},{12,8},{1,5},{5,1},{9,13},{13,9},{2,6},{6,2},{1... | collective-permute-start | bytes 1572872 | tf_op jit(solution)/shard_map/ppermute | solution.py:466
  121.9 24.2 %collective-permute-start.16 = (bf16[128,2048]{1,0:T(8,128)(2,1)}, bf16[128,2048]{1,0:T(8,128)(2,1)}, u32[]{:S(2)}, u32[]{:S(2)}) collective-permute-start(bf16[128,2048]{1,0:T(8,128)(2,1)} %collective-permute-done.15.rest_4_), channel_id=1, source_target_pairs={{0,4},{4,0},{8,12},{12,8},{1,5},{5,1},{9,13},{13,9},{2,6},{6,2},{1... | collective-permute-start | bytes 1572872 | tf_op jit(solution)/shard_map/ppermute | solution.py:466
  135.1 24.1 %collective-permute-start.17 = (bf16[128,2048]{1,0:T(8,128)(2,1)}, bf16[128,2048]{1,0:T(8,128)(2,1)S(1)}, u32[]{:S(2)}, u32[]{:S(2)}) collective-permute-start(bf16[128,2048]{1,0:T(8,128)(2,1)} %collective-permute-done.13.rest_2_), channel_id=1, source_target_pairs={{0,1},{1,0},{2,3},{3,2},{4,5},{5,4},{6,7},{7,6},{8,9},{9,8},{10,11... | collective-permute-start | bytes 1572872 | tf_op jit(solution)/shard_map/ppermute | solution.py:466
  135.5 23.9 %collective-permute-start.19 = (bf16[128,2048]{1,0:T(8,128)(2,1)}, bf16[128,2048]{1,0:T(8,128)(2,1)}, u32[]{:S(2)}, u32[]{:S(2)}) collective-permute-start(bf16[128,2048]{1,0:T(8,128)(2,1)} %collective-permute-done.15.rest_4_), channel_id=1, source_target_pairs={{0,1},{1,0},{2,3},{3,2},{4,5},{5,4},{6,7},{7,6},{8,9},{9,8},{10,11... | collective-permute-start | bytes 1572872 | tf_op jit(solution)/shard_map/ppermute | solution.py:466
  146.1 13.3 %collective-permute-start.18 = (bf16[128,2048]{1,0:T(8,128)(2,1)}, bf16[128,2048]{1,0:T(8,128)(2,1)}, u32[]{:S(2)}, u32[]{:S(2)}) collective-permute-start(bf16[128,2048]{1,0:T(8,128)(2,1)} %collective-permute-done.14.rest_3_), channel_id=1, source_target_pairs={{0,1},{1,0},{2,3},{3,2},{4,5},{5,4},{6,7},{7,6},{8,9},{9,8},{10,11... | collective-permute-start | bytes 1572872 | tf_op jit(solution)/shard_map/ppermute | solution.py:466
  146.1 13.3 %collective-permute-start.20 = (bf16[128,2048]{1,0:T(8,128)(2,1)}, bf16[128,2048]{1,0:T(8,128)(2,1)}, u32[]{:S(2)}, u32[]{:S(2)}) collective-permute-start(bf16[128,2048]{1,0:T(8,128)(2,1)} %collective-permute-done.16.rest_5_), channel_id=1, source_target_pairs={{0,1},{1,0},{2,3},{3,2},{4,5},{5,4},{6,7},{7,6},{8,9},{9,8},{10,11... | collective-permute-start | bytes 1572872 | tf_op jit(solution)/shard_map/ppermute | solution.py:466
  (5 other events, 116.3 us)
where the time goes:
time: 600 us; the launch traced here: 599 us
  Pallas kernels  494 us (82%)
  waiting for transfers between devices  74.2 us (12%)
  starting transfers between devices  15.1 us (3%)
  local copies, waits for them, and re-layouts  13.1 us (2%)
    pallas_call x1, Pallas kernels, mlp_call(): pl.pallas_call(mlp_kernel, in_specs=[ANY] * 7, out_specs=[ANY] * len(outs...  398 us
    ppermute x24, waiting for transfers between devices, swap(): lax.ppermute(a, axis, [(i, i ^ bit) for i in range(mesh.shape[axis])])  74.2 us
    pallas_call x2, Pallas kernels, out_call(): pl.pallas_call(out_kernel, grid=(count // step,), in_specs=[SMEM, pl.Bloc...  33.3 us
    pallas_call x2, Pallas kernels, query_call(): pl.pallas_call(functools.partial(kernel, head_dim), grid=(nb // step,), i...  25.8 us
    pallas_call x2, Pallas kernels, attn_call(): pl.pallas_call(functools.partial(attn_kernel, base), grid=(count,), in_sp...  25.5 us
    ppermute x24, starting transfers between devices, swap(): lax.ppermute(a, axis, [(i, i ^ bit) for i in range(mesh.shape[axis])])  15.1 us
  transfers between devices with their start and end apart: 24, of which 7 were waited for; matrix products, arithmetic and copies ran while one was open for 1% of the time, Pallas kernels for 10%

commit v1 on v0

--- a/solution.py
+++ b/solution.py
@@ -176,7 +176,8 @@
     )(*args)
 
 
-def attn_kernel(base, pos_ref, pre_ref, val_ref, qa_ref, qb_ref, kv0, kv1, kv2, kv3, o_ref, k_scr, v_scr):
+def attn_kernel(base, pos_ref, pre_ref, val_ref, qa_ref, qb_ref, kv0, kv1, kv2, kv3, *rest):
+    o_ref, k_scr, v_scr = rest[-3:]
     _, heads, rows, hd = qa_ref.shape
     b = pl.program_id(0) + base
     for p, kv_ref in enumerate((kv0, kv1, kv2, kv3)):
@@ -206,22 +207,23 @@
             head += 2
 
 
-def attn_call(base, count, pos, prefix_len, valid_len, qa, qb, kvs):
-    _, heads, rows, hd = qa.shape
+def attn_call(base, count, pos, prefix_len, valid_len, qa, qb, kvs, into=None):
+    nb, heads, rows, hd = qa.shape
     d = 2 * heads * hd
     q_spec = pl.BlockSpec((1, heads, rows, hd), lambda i: (i + base, 0, 0, 0))
     kv_spec = pl.BlockSpec((1, rows, 2 * hd), lambda i: (i, 0, 0))
     return pl.pallas_call(
         functools.partial(attn_kernel, base),
         grid=(count,),
-        in_specs=[SMEM] * 3 + [q_spec] * 2 + [kv_spec] * 4,
-        out_specs=pl.BlockSpec((1, rows, d), lambda i: (i, 0, 0)),
-        out_shape=jax.ShapeDtypeStruct((count, rows, d), jnp.bfloat16),
+        in_specs=[SMEM] * 3 + [q_spec] * 2 + [kv_spec] * 4 + [ANY] * (into is not None),
+        out_specs=pl.BlockSpec((1, rows, d), lambda i: (i + base, 0, 0)),
+        out_shape=jax.ShapeDtypeStruct((nb, rows, d), jnp.bfloat16),
+        input_output_aliases={} if into is None else {9: 0},
         scratch_shapes=[pltpu.VMEM((4 * rows, hd), jnp.bfloat16)] * 2,
         compiler_params=params(VMEM_MIB),
         cost_estimate=cost(4 * count * 2 * heads * rows * 4 * rows * hd * 2, 8 * count * rows * d),
         name="attention",
-    )(pos, prefix_len, valid_len, qa, qb, *kvs)
+    )(pos, prefix_len, valid_len, qa, qb, *kvs, *(() if into is None else (into,)))
 
 
 def out_kernel(group_ref, o_ref, h_ref, *rest):
@@ -265,9 +267,11 @@
     )(group, o, hidden, *weights, gain)
 
 
-def mlp_kernel(xa_hbm, xb_hbm, mid_a, mid_b, wg0, wu0, wd0, out_hbm, wg1, wu1, wd1, in_a, in_b, send_a, send_b, ret_a, ret_b,
+def mlp_kernel(x_hbm, mid_hbm, wg0, wu0, wd0, out_hbm, wg1, wu1, wd1, in_a, in_b, send_a, send_b, ret_a, ret_b,
                xbuf, own, acc, stage, mid, their, gb, ub, db, sems, sem_x, sem_in, sem_out, far_send, far_recv, row_send, row_recv):
-    m, _ = xa_hbm.shape
+    m, _ = in_a.shape
+    xa_hbm, xb_hbm = x_hbm.at[pl.ds(0, m)], x_hbm.at[pl.ds(m, m)]
+    mid_a, mid_b = mid_hbm.at[pl.ds(0, m)], mid_hbm.at[pl.ds(m, m)]
     tiles = wg0.shape[1] // F_TILE
     steps = 8 * tiles
     starts = (0, tiles, 2 * tiles, 4 * tiles, 6 * tiles, 7 * tiles)
@@ -275,6 +279,10 @@
     size = lax.axis_size("tp")
     chip = lax.rem(me + size // 2, size)
     core = me + 1 - 2 * lax.rem(me, 2)
+
+    pltpu.make_async_copy(xa_hbm, xbuf.at[0], sem_x.at[0]).start()
+    for ws, buf, i in ((wg0.at[:, pl.ds(0, F_TILE)], gb, 0), (wu0.at[:, pl.ds(0, F_TILE)], ub, 1), (wd0.at[pl.ds(0, F_TILE), :], db, 2)):
+        pltpu.make_async_copy(ws, buf.at[0], sems.at[0, i]).start()
 
     barrier = pltpu.get_barrier_semaphore()
     for peer in (chip, core):
@@ -322,8 +330,6 @@
     def x_copy(src, slot):
         return pltpu.make_async_copy(src, xbuf.at[slot], sem_x.at[slot])
 
-    x_copy(xa_hbm, 0).start()
-    start(jnp.int32(0), 0)
     acc[...] = jnp.zeros_like(acc)
     x_sources = (xa_hbm, xb_hbm, in_a, in_b, xa_hbm, xb_hbm)
     chunk = ROW_BLOCK // 2
@@ -411,11 +417,11 @@
         for k in (4, 5):
             @pl.when(j == starts[k] + tiles - 1)
             def _():
-                ret, mid_hbm = ((ret_a, mid_a), (ret_b, mid_b))[k - 4]
+                ret, mid_k = ((ret_a, mid_a), (ret_b, mid_b))[k - 4]
                 rows[k - 2].wait_recv()
                 got = pltpu.make_async_copy(ret, their, sem_in.at[1])
                 got.start()
-                pltpu.make_async_copy(mid_hbm, mid, sem_in.at[0]).wait()
+                pltpu.make_async_copy(mid_k, mid, sem_in.at[0]).wait()
                 got.wait()
                 if k == 5:
                     pltpu.make_async_copy(stage, out_hbm.at[pl.ds(0, m)], sem_out.at[1]).wait()
@@ -434,15 +440,15 @@
         c.wait_send()
 
 
-def mlp_call(x_a, x_b, mid_a, mid_b, weights):
-    m, d = x_a.shape
+def mlp_call(x, mid, weights):
+    m, d = x.shape[0] // 2, x.shape[1]
     f = weights[0].shape[1]
     half = jax.ShapeDtypeStruct((m, d), jnp.bfloat16)
     outs = [jax.ShapeDtypeStruct((2 * m, d), jnp.bfloat16)] + [jax.ShapeDtypeStruct(w.shape, w.dtype) for w in weights] + [half] * 6
     dma = pltpu.SemaphoreType.DMA
     return pl.pallas_call(
         mlp_kernel,
-        in_specs=[ANY] * 7,
+        in_specs=[ANY] * 5,
         out_specs=[ANY] * len(outs),
         out_shape=outs,
         scratch_shapes=[
@@ -454,7 +460,25 @@
         compiler_params=params(60, collective_id=0, has_side_effects=True),
         cost_estimate=cost(48 * m * d * f, 48 * d * f),
         name="mlp",
-    )(x_a, x_b, mid_a, mid_b, *weights)[0]
+    )(x, mid, *weights)[0]
+
+
+def copy_kernel(src_ref, dst_ref):
+    dst_ref[...] = src_ref[...]
+
+
+def copy_call(a):
+    blk = pl.BlockSpec((ROW_BLOCK // 2, a.shape[1]), lambda i: (i, 0))
+    return pl.pallas_call(
+        copy_kernel,
+        grid=(2 * a.shape[0] // ROW_BLOCK,),
+        in_specs=[blk],
+        out_specs=blk,
+        out_shape=jax.ShapeDtypeStruct(a.shape, a.dtype),
+        compiler_params=params(60),
+        cost_estimate=cost(a.size, 4 * a.size),
+        name="result",
+    )(a)
 
 
 def solution(mesh):
@@ -499,13 +523,11 @@
         w_outs = [w_out, swap(w_out, "tp", 1)] + gather(wo_got, False)
         near = (w_gate, w_up, w_down)
 
-        mids, mine = [], []
+        o = None
         for base, kv in ((0, kvs[0]), (half, kvs[1])):
-            o = attn_call(base, half, pos, prefix_len, valid_len, query_a, query_b, kv)
-            mid, x = out_call(base, o, hidden, group, w_outs, norm_mlp[None])
-            mids.append(mid)
-            mine.append(x)
-        out = mlp_call(*mine, *mids, near)
+            o = attn_call(base, half, pos, prefix_len, valid_len, query_a, query_b, kv, o)
+        mid, x = out_call(0, o, hidden, group, w_outs, norm_mlp[None])
+        out = copy_call(mlp_call(x, mid, near))
         return out.reshape(nb, rows, d), key_local, value_local
 
     return jax.shard_map(local_layer, mesh=mesh, in_specs=arg_specs, out_specs=(row_spec, row_spec, row_spec), check_vma=False)

time: 600 us -> 592 us (0.987)
  local copies, waits for them, and re-layouts: 13.1 us -> 5.63 us
    unnamed x11 -> x10, local copies, waits for them, and re-layouts: 8.28 us -> 0.76 us
    pallas_call x2 -> x1, Pallas kernels: 33.3 us -> 25.9 us  [out_call(): pl.pallas_call(out_kernel, grid=(count // step,), in_specs=[SMEM, pl.Bloc...]
    pallas_call x1 -> x2, Pallas kernels: 398 us -> 405 us  [the longest x1 397 us: mlp_call(): pl.pallas_call(mlp_kernel, in_specs=[ANY] * 5, out_specs=[ANY] * len(outs...]
  transfers between devices with their start and end apart: 24 -> 24, of which waited for: 7 -> 7; matrix products, arithmetic and copies ran while one was open for 1% -> 1% of each run, Pallas kernels for 10% -> 11%
where the time goes in v1:
time: 592 us; the launch traced here: 591 us
  Pallas kernels  494 us (83%)
  waiting for transfers between devices  74.4 us (13%)
  starting transfers between devices  15 us (3%)
    pallas_call x1, Pallas kernels, mlp_call(): pl.pallas_call(mlp_kernel, in_specs=[ANY] * 5, out_specs=[ANY] * len(outs...  397 us
    ppermute x24, waiting for transfers between devices, swap(): lax.ppermute(a, axis, [(i, i ^ bit) for i in range(mesh.shape[axis])])  74.4 us
    pallas_call x1, Pallas kernels, out_call(): pl.pallas_call(out_kernel, grid=(count // step,), in_specs=[SMEM, pl.Bloc...  25.9 us
    pallas_call x2, Pallas kernels, query_call(): pl.pallas_call(functools.partial(kernel, head_dim), grid=(nb // step,), i...  25.8 us
    pallas_call x2, Pallas kernels, attn_call(): pl.pallas_call(functools.partial(attn_kernel, base), grid=(count,), in_sp...  25.5 us
    ppermute x24, starting transfers between devices, swap(): lax.ppermute(a, axis, [(i, i ^ bit) for i in range(mesh.shape[axis])])  15 us
  transfers between devices with their start and end apart: 24, of which 7 were waited for; matrix products, arithmetic and copies ran while one was open for 1% of the time, Pallas kernels for 11%

profile of v1, /device:TPU:0, one launch (start us, length us, event | category | flops | bytes accessed | tf_op | source)
XLA Modules:
  0.0 591.4 jit_solution(10212489614941101335)
XLA Ops:
  0.6 1.1 constant_dynamic-slice_fusion
  1.7 3.2 collective-permute-start.16
  5.0 1.9 constant_dynamic-slice_fusion.1
  7.0 1.3 broadcast_in_dim.8.gain_ref
  8.2 0.9 multiply_sine_fusion
  9.2 11.1 %kv_proj.1 = (bf16[16,112,2048]{2,1,0:T(8,128)(2,1)}, bf16[16,112,256]{2,1,0:T(8,128)(2,1)}, bf16[16,112,256]{2,1,0:T(8,128)(2,1)}, bf16[8,112,512]{2,1,0:T(8,128)(2,1)}, bf16[8,112,512]{2,1,0:T(8,128)(2,1)}) custom-call(bf16[16,112,2048]{2,1,0:T(8,128)(2,1)} %h_ref.3, bf16[1,2048]{1,0:T(2,128)(2,1)} %broadcast_in_dim.8.gain_ref, bf16[2048,256]{1,0:T(8,128)(2,1)} %wk_ref.1, ...), custom_call_target="tpu_custom_call" | custom-call | flops 3758096384 | bytes 14680064 | tf_op jit(solution)/shard_map/kv_proj/pallas_call | solution.py:92
  20.2 2.0 collective-permute-start.10
  22.3 6.8 %collective-permute-done.1.rest_0_ = bf16[512,512]{1,0:T(8,128)(2,1)} collective-permute-done((bf16[512,512]{1,0:T(8,128)(2,1)}, bf16[512,512]{1,0:T(8,128)(2,1)}, u32[]{:S(2)}, u32[]{:S(2)}) %collective-permute-start.1) | collective-permute-done | bytes 524320 | tf_op jit(solution)/shard_map/ppermute | solution.py:490
  29.1 2.0 collective-permute-start.2
  31.1 17.6 %collective-permute-done.10.kv2 = bf16[8,112,512]{2,1,0:T(8,128)(2,1)} collective-permute-done((bf16[8,112,512]{2,1,0:T(8,128)(2,1)}, bf16[8,112,512]{2,1,0:T(8,128)(2,1)}, u32[]{:S(2)}, u32[]{:S(2)}) %collective-permute-start.10) | collective-permute-done | bytes 917536 | tf_op jit(solution)/shard_map/ppermute | solution.py:490
  48.7 18.8 %collective-permute-done.13.kv2 = bf16[8,112,512]{2,1,0:T(8,128)(2,1)} collective-permute-done((bf16[8,112,512]{2,1,0:T(8,128)(2,1)}, bf16[8,112,512]{2,1,0:T(8,128)(2,1)}, u32[]{:S(2)}, u32[]{:S(2)}) %collective-permute-start.13) | collective-permute-done | bytes 917536 | tf_op jit(solution)/shard_map/ppermute | solution.py:490
  67.5 1.8 collective-permute-start.3
  71.8 10.9 %collective-permute-done.3.rest_2_ = bf16[512,512]{1,0:T(8,128)(2,1)} collective-permute-done((bf16[512,512]{1,0:T(8,128)(2,1)}, bf16[512,512]{1,0:T(8,128)(2,1)}, u32[]{:S(2)}, u32[]{:S(2)}) %collective-permute-start.3) | collective-permute-done | bytes 524320 | tf_op jit(solution)/shard_map/ppermute | solution.py:490
  82.7 9.5 %collective-permute-done.4.rest_3_ = bf16[512,512]{1,0:T(8,128)(2,1)} collective-permute-done((bf16[512,512]{1,0:T(8,128)(2,1)}, bf16[512,512]{1,0:T(8,128)(2,1)}, u32[]{:S(2)}, u32[]{:S(2)}) %collective-permute-start.4) | collective-permute-done | bytes 524320 | tf_op jit(solution)/shard_map/ppermute | solution.py:490
  92.7 12.3 %query_near.1.qa_ref = bf16[16,4,112,256]{3,2,1,0:T(8,128)(2,1)} custom-call(bf16[16,112,2048]{2,1,0:T(8,128)(2,1)} %get-tuple-element.11.x_ref, bf16[2048,512]{1,0:T(8,128)(2,1)} %w0_ref.1, bf16[2048,512]{1,0:T(8,128)(2,1)} %collective-permute-done.w1_ref, f32[112,128]{1,0:T(8,128)} %get-tuple-element.20.cos_ref.rest_8_, ...), custom_call_target="tpu_custom_call" | custom-call | flops 7516192768 | bytes 7340032 | tf_op jit(solution)/shard_map/query_near/pallas_call | solution.py:166
  105.1 1.6 collective-permute-start.18
  106.9 13.4 %query_far.1.qb_ref = bf16[16,4,112,256]{3,2,1,0:T(8,128)(2,1)} custom-call(s32[4]{0:T(128)} %iota_xor_fusion.group_ref, bf16[16,112,2048]{2,1,0:T(8,128)(2,1)} %get-tuple-element.11.x_ref, bf16[512,512]{1,0:T(8,128)(2,1)} %collective-permute-done.1.rest_0_, bf16[512,512]{1,0:T(8,128)(2,1)} %collective-permute-done.2.rest_1_, ...), custom_call_target="tpu_custom_call" | custom-call | flops 7516192768 | bytes 7340032 | tf_op jit(solution)/shard_map/query_far/pallas_call | solution.py:166
  120.3 1.6 collective-permute-start.17
  122.4 12.7 %attention.2.rest_0_ = bf16[16,112,2048]{2,1,0:T(8,128)(2,1)} custom-call(s32[4]{0:T(128)} %xor_multiply_fusion.pos_ref, s32[16]{0:T(128)} %pre_ref.3, s32[16]{0:T(128)} %val_ref.3, bf16[16,4,112,256]{3,2,1,0:T(8,128)(2,1)} %query_near.1.qa_ref, bf16[16,4,112,256]{3,2,1,0:T(8,128)(2,1)} %query_far.1.qb_ref, bf16[8,112,512]{2,1,0:T(8,128)(2,1)} %get-tuple-element.13.kv0, ...), custom_call_target="tpu_custom_call" | custom-call | flops 6576668672 | bytes 14680064 | tf_op jit(solution)/shard_map/attention/pallas_call | solution.py:215
  135.7 10.4 %collective-permute-done.19.rest_5_ = bf16[128,2048]{1,0:T(8,128)(2,1)} collective-permute-done((bf16[128,2048]{1,0:T(8,128)(2,1)}, bf16[128,2048]{1,0:T(8,128)(2,1)}, u32[]{:S(2)}, u32[]{:S(2)}) %collective-permute-start.19) | collective-permute-done | bytes 524320 | tf_op jit(solution)/shard_map/ppermute | solution.py:490
  146.6 12.8 %attention.3.o_ref = bf16[16,112,2048]{2,1,0:T(8,128)(2,1)} custom-call(s32[4]{0:T(128)} %xor_multiply_fusion.pos_ref, s32[16]{0:T(128)} %pre_ref.3, s32[16]{0:T(128)} %val_ref.3, bf16[16,4,112,256]{3,2,1,0:T(8,128)(2,1)} %query_near.1.qa_ref, bf16[16,4,112,256]{3,2,1,0:T(8,128)(2,1)} %query_far.1.qb_ref, ...), custom_call_target="tpu_custom_call", output_to_operand_aliasing={{}: (9, {})} | custom-call | flops 6576668672 | bytes 14680064 | tf_op jit(solution)/shard_map/attention/pallas_call | solution.py:215
  160.1 25.9 %out_proj.1 = (bf16[1792,2048]{1,0:T(8,128)(2,1)}, bf16[1792,2048]{1,0:T(8,128)(2,1)}) custom-call(s32[4]{0:T(128)} %iota_xor_fusion.group_ref, bf16[16,112,2048]{2,1,0:T(8,128)(2,1)} %attention.3.o_ref, bf16[16,112,2048]{2,1,0:T(8,128)(2,1)} %h_ref.3, bf16[512,2048]{1,0:T(8,128)(2,1)} %rest_0_.1, bf16[512,2048]{1,0:T(8,128)(2,1)} %collective-permute-done.15.rest_1_, ...), custom_call_target="tpu_custom_call" | custom-call | flops 15032385536 | bytes 29360128 | tf_op jit(solution)/shard_map/out_proj/pallas_call | solution.py:255
  186.0 397.0 %mlp.1 = (bf16[1792,2048]{1,0:T(8,128)(2,1)}, bf16[2048,4096]{1,0:T(8,128)(2,1)}, bf16[2048,4096]{1,0:T(8,128)(2,1)}, bf16[4096,2048]{1,0:T(8,128)(2,1)}, bf16[8...) custom-call(bf16[1792,2048]{1,0:T(8,128)(2,1)} %get-tuple-element.14, ...), custom_call_target="tpu_custom_call" | custom-call | flops 360777252864 | bytes 402653184 | tf_op jit(solution)/shard_map/mlp/pallas_call | solution.py:449
  583.0 8.4 %result.1 = bf16[1792,2048]{1,0:T(8,128)(2,1)} custom-call(bf16[1792,2048]{1,0:T(8,128)(2,1)} %get-tuple-element.16.src_ref), custom_call_target="tpu_custom_call" | custom-call | flops 3670016 | bytes 14680064 | tf_op jit(solution)/shard_map/result/pallas_call | solution.py:472
  (51 shorter events, 5.6 us)
Async XLA Ops:
  1.7 29.4 %collective-permute-start.16 = (bf16[128,2048]{1,0:T(8,128)(2,1)S(1)}, bf16[128,2048]{1,0:T(8,128)(2,1)}, u32[]{:S(2)}, u32[]{:S(2)}) collective-permute-start(bf16[128,2048]{1,0:T(8,128)(2,1)S(1)} %constant_dynamic-slice_fusion), channel_id=1, source_target_pairs={{0,2},{1,3},{2,0},{3,1},{4,6},{5,7},{6,4},{7,5},{8,10},{9,11},{10,... | collective-permute-start | bytes 1572872 | tf_op jit(solution)/shard_map/ppermute | solution.py:490
  5.0 87.2 %collective-permute-start = (bf16[2048,512]{1,0:T(8,128)(2,1)}, bf16[2048,512]{1,0:T(8,128)(2,1)}, u32[]{:S(2)}, u32[]{:S(2)}) collective-permute-start(bf16[2048,512]{1,0:T(8,128)(2,1)} %w0_ref.1), channel_id=1, source_target_pairs={{0,1},{1,0},{2,3},{3,2},{4,5},{5,4},{6,7},{7,6},{8,9},{9,8},{10,11... | collective-permute-start | bytes 6291464 | tf_op jit(solution)/shard_map/ppermute | solution.py:490
  6.9 22.2 %collective-permute-start.1 = (bf16[512,512]{1,0:T(8,128)(2,1)}, bf16[512,512]{1,0:T(8,128)(2,1)}, u32[]{:S(2)}, u32[]{:S(2)}) collective-permute-start(bf16[512,512]{1,0:T(8,128)(2,1)} %constant_dynamic-slice_fusion.1), channel_id=1, source_target_pairs={{0,2},{1,3},{2,0},{3,1},{4,6},{5,7},{6,4},{7,5},{8,10},{9,11},{10,... | collective-permute-start | bytes 1572872 | tf_op jit(solution)/shard_map/ppermute | solution.py:490
  20.2 28.5 %collective-permute-start.10 = (bf16[8,112,512]{2,1,0:T(8,128)(2,1)}, bf16[8,112,512]{2,1,0:T(8,128)(2,1)}, u32[]{:S(2)}, u32[]{:S(2)}) collective-permute-start(bf16[8,112,512]{2,1,0:T(8,128)(2,1)} %get-tuple-element.12.kv0), channel_id=1, source_target_pairs={{0,2},{1,3},{2,0},{3,1},{4,6},{5,7},{6,4},{7,5},{8,10},{9,11},{10,... | collective-permute-start | bytes 2752520 | tf_op jit(solution)/shard_map/ppermute | solution.py:490
  22.2 45.3 %collective-permute-start.13 = (bf16[8,112,512]{2,1,0:T(8,128)(2,1)}, bf16[8,112,512]{2,1,0:T(8,128)(2,1)}, u32[]{:S(2)}, u32[]{:S(2)}) collective-permute-start(bf16[8,112,512]{2,1,0:T(8,128)(2,1)} %get-tuple-element.13.kv0), channel_id=1, source_target_pairs={{0,2},{1,3},{2,0},{3,1},{4,6},{5,7},{6,4},{7,5},{8,10},{9,11},{10,... | collective-permute-start | bytes 2752520 | tf_op jit(solution)/shard_map/ppermute | solution.py:490
  29.1 40.3 %collective-permute-start.2 = (bf16[512,512]{1,0:T(8,128)(2,1)}, bf16[512,512]{1,0:T(8,128)(2,1)}, u32[]{:S(2)}, u32[]{:S(2)}) collective-permute-start(bf16[512,512]{1,0:T(8,128)(2,1)} %collective-permute-done.1.rest_0_), channel_id=1, source_target_pairs={{0,4},{4,0},{8,12},{12,8},{1,5},{5,1},{9,13},{13,9},{2,6},{6,2},{1... | collective-permute-start | bytes 1572872 | tf_op jit(solution)/shard_map/ppermute | solution.py:490
  31.1 40.1 %collective-permute-start.12 = (bf16[8,112,512]{2,1,0:T(8,128)(2,1)}, bf16[8,112,512]{2,1,0:T(8,128)(2,1)S(1)}, u32[]{:S(2)}, u32[]{:S(2)}) collective-permute-start(bf16[8,112,512]{2,1,0:T(8,128)(2,1)} %get-tuple-element.13.kv0), channel_id=1, source_target_pairs={{0,1},{1,0},{2,3},{3,2},{4,5},{5,4},{6,7},{7,6},{8,9},{9,8},{10,11... | collective-permute-start | bytes 2752520 | tf_op jit(solution)/shard_map/ppermute | solution.py:490
  48.7 22.5 %collective-permute-start.5 = (bf16[512,512]{1,0:T(8,128)(2,1)}, bf16[512,512]{1,0:T(8,128)(2,1)S(1)}, u32[]{:S(2)}, u32[]{:S(2)}) collective-permute-start(bf16[512,512]{1,0:T(8,128)(2,1)} %collective-permute-done.1.rest_0_), channel_id=1, source_target_pairs={{0,1},{1,0},{2,3},{3,2},{4,5},{5,4},{6,7},{7,6},{8,9},{9,8},{10,11... | collective-permute-start | bytes 1572872 | tf_op jit(solution)/shard_map/ppermute | solution.py:490
  67.5 15.1 %collective-permute-start.3 = (bf16[512,512]{1,0:T(8,128)(2,1)}, bf16[512,512]{1,0:T(8,128)(2,1)}, u32[]{:S(2)}, u32[]{:S(2)}) collective-permute-start(bf16[512,512]{1,0:T(8,128)(2,1)} %collective-permute-done.1.rest_0_), channel_id=1, source_target_pairs={{0,8},{4,12},{8,0},{12,4},{1,9},{5,13},{9,1},{13,5},{2,10},{6,14},... | collective-permute-start | bytes 1572872 | tf_op jit(solution)/shard_map/ppermute | solution.py:490
  69.4 22.8 %collective-permute-start.4 = (bf16[512,512]{1,0:T(8,128)(2,1)}, bf16[512,512]{1,0:T(8,128)(2,1)}, u32[]{:S(2)}, u32[]{:S(2)}) collective-permute-start(bf16[512,512]{1,0:T(8,128)(2,1)} %collective-permute-done.2.rest_1_), channel_id=1, source_target_pairs={{0,8},{4,12},{8,0},{12,4},{1,9},{5,13},{9,1},{13,5},{2,10},{6,14},... | collective-permute-start | bytes 1572872 | tf_op jit(solution)/shard_map/ppermute | solution.py:490
  71.2 88.2 %collective-permute-start.15 = (bf16[512,2048]{1,0:T(8,128)(2,1)}, bf16[512,2048]{1,0:T(8,128)(2,1)}, u32[]{:S(2)}, u32[]{:S(2)}) collective-permute-start(bf16[512,2048]{1,0:T(8,128)(2,1)} %rest_0_.1), channel_id=1, source_target_pairs={{0,1},{1,0},{2,3},{3,2},{4,5},{5,4},{6,7},{7,6},{8,9},{9,8},{10,11... | collective-permute-start | bytes 6291464 | tf_op jit(solution)/shard_map/ppermute | solution.py:490
  71.3 50.6 %collective-permute-start.14 = (bf16[8,112,512]{2,1,0:T(8,128)(2,1)}, bf16[8,112,512]{2,1,0:T(8,128)(2,1)}, u32[]{:S(2)}, u32[]{:S(2)}) collective-permute-start(bf16[8,112,512]{2,1,0:T(8,128)(2,1)} %collective-permute-done.13.kv2), channel_id=1, source_target_pairs={{0,1},{1,0},{2,3},{3,2},{4,5},{5,4},{6,7},{7,6},{8,9},{9,8},{10,11... | collective-permute-start | bytes 2752520 | tf_op jit(solution)/shard_map/ppermute | solution.py:490
  82.7 22.5 %collective-permute-start.6 = (bf16[512,512]{1,0:T(8,128)(2,1)}, bf16[512,512]{1,0:T(8,128)(2,1)}, u32[]{:S(2)}, u32[]{:S(2)}) collective-permute-start(bf16[512,512]{1,0:T(8,128)(2,1)} %collective-permute-done.2.rest_1_), channel_id=1, source_target_pairs={{0,1},{1,0},{2,3},{3,2},{4,5},{5,4},{6,7},{7,6},{8,9},{9,8},{10,11... | collective-permute-start | bytes 1572872 | tf_op jit(solution)/shard_map/ppermute | solution.py:490
  92.2 12.9 %collective-permute-start.7 = (bf16[512,512]{1,0:T(8,128)(2,1)}, bf16[512,512]{1,0:T(8,128)(2,1)}, u32[]{:S(2)}, u32[]{:S(2)}) collective-permute-start(bf16[512,512]{1,0:T(8,128)(2,1)} %collective-permute-done.3.rest_2_), channel_id=1, source_target_pairs={{0,1},{1,0},{2,3},{3,2},{4,5},{5,4},{6,7},{7,6},{8,9},{9,8},{10,11... | collective-permute-start | bytes 1572872 | tf_op jit(solution)/shard_map/ppermute | solution.py:490
  92.2 14.5 %collective-permute-start.8 = (bf16[512,512]{1,0:T(8,128)(2,1)}, bf16[512,512]{1,0:T(8,128)(2,1)}, u32[]{:S(2)}, u32[]{:S(2)}) collective-permute-start(bf16[512,512]{1,0:T(8,128)(2,1)} %collective-permute-done.4.rest_3_), channel_id=1, source_target_pairs={{0,1},{1,0},{2,3},{3,2},{4,5},{5,4},{6,7},{7,6},{8,9},{9,8},{10,11... | collective-permute-start | bytes 1572872 | tf_op jit(solution)/shard_map/ppermute | solution.py:490
  105.1 30.0 %collective-permute-start.9 = (bf16[8,112,512]{2,1,0:T(8,128)(2,1)S(1)}, bf16[8,112,512]{2,1,0:T(8,128)(2,1)}, u32[]{:S(2)}, u32[]{:S(2)}) collective-permute-start(bf16[8,112,512]{2,1,0:T(8,128)(2,1)S(1)} %copy-done), channel_id=1, source_target_pairs={{0,1},{1,0},{2,3},{3,2},{4,5},{5,4},{6,7},{7,6},{8,9},{9,8},{10,11... | collective-permute-start | bytes 2752520 | tf_op jit(solution)/shard_map/ppermute | solution.py:490
  105.1 15.2 %collective-permute-start.18 = (bf16[128,2048]{1,0:T(8,128)(2,1)}, bf16[128,2048]{1,0:T(8,128)(2,1)}, u32[]{:S(2)}, u32[]{:S(2)}) collective-permute-start(bf16[128,2048]{1,0:T(8,128)(2,1)} %collective-permute-done.16.rest_2_), channel_id=1, source_target_pairs={{0,8},{4,12},{8,0},{12,4},{1,9},{5,13},{9,1},{13,5},{2,10},{6,14},... | collective-permute-start | bytes 1572872 | tf_op jit(solution)/shard_map/ppermute | solution.py:490
  106.7 39.4 %collective-permute-start.11 = (bf16[8,112,512]{2,1,0:T(8,128)(2,1)}, bf16[8,112,512]{2,1,0:T(8,128)(2,1)}, u32[]{:S(2)}, u32[]{:S(2)}) collective-permute-start(bf16[8,112,512]{2,1,0:T(8,128)(2,1)} %collective-permute-done.10.kv2), channel_id=1, source_target_pairs={{0,1},{1,0},{2,3},{3,2},{4,5},{5,4},{6,7},{7,6},{8,9},{9,8},{10,11... | collective-permute-start | bytes 2752520 | tf_op jit(solution)/shard_map/ppermute | solution.py:490
  120.3 15.1 %collective-permute-start.17 = (bf16[128,2048]{1,0:T(8,128)(2,1)}, bf16[128,2048]{1,0:T(8,128)(2,1)}, u32[]{:S(2)}, u32[]{:S(2)}) collective-permute-start(bf16[128,2048]{1,0:T(8,128)(2,1)} %collective-permute-done.16.rest_2_), channel_id=1, source_target_pairs={{0,4},{4,0},{8,12},{12,8},{1,5},{5,1},{9,13},{13,9},{2,6},{6,2},{1... | collective-permute-start | bytes 1572872 | tf_op jit(solution)/shard_map/ppermute | solution.py:490
  121.9 24.2 %collective-permute-start.19 = (bf16[128,2048]{1,0:T(8,128)(2,1)}, bf16[128,2048]{1,0:T(8,128)(2,1)}, u32[]{:S(2)}, u32[]{:S(2)}) collective-permute-start(bf16[128,2048]{1,0:T(8,128)(2,1)} %collective-permute-done.18.rest_4_), channel_id=1, source_target_pairs={{0,4},{4,0},{8,12},{12,8},{1,5},{5,1},{9,13},{13,9},{2,6},{6,2},{1... | collective-permute-start | bytes 1572872 | tf_op jit(solution)/shard_map/ppermute | solution.py:490
  135.1 24.2 %collective-permute-start.20 = (bf16[128,2048]{1,0:T(8,128)(2,1)}, bf16[128,2048]{1,0:T(8,128)(2,1)S(1)}, u32[]{:S(2)}, u32[]{:S(2)}) collective-permute-start(bf16[128,2048]{1,0:T(8,128)(2,1)} %collective-permute-done.16.rest_2_), channel_id=1, source_target_pairs={{0,1},{1,0},{2,3},{3,2},{4,5},{5,4},{6,7},{7,6},{8,9},{9,8},{10,11... | collective-permute-start | bytes 1572872 | tf_op jit(solution)/shard_map/ppermute | solution.py:490
  135.5 23.9 %collective-permute-start.22 = (bf16[128,2048]{1,0:T(8,128)(2,1)}, bf16[128,2048]{1,0:T(8,128)(2,1)}, u32[]{:S(2)}, u32[]{:S(2)}) collective-permute-start(bf16[128,2048]{1,0:T(8,128)(2,1)} %collective-permute-done.18.rest_4_), channel_id=1, source_target_pairs={{0,1},{1,0},{2,3},{3,2},{4,5},{5,4},{6,7},{7,6},{8,9},{9,8},{10,11... | collective-permute-start | bytes 1572872 | tf_op jit(solution)/shard_map/ppermute | solution.py:490
  146.1 13.3 %collective-permute-start.21 = (bf16[128,2048]{1,0:T(8,128)(2,1)}, bf16[128,2048]{1,0:T(8,128)(2,1)}, u32[]{:S(2)}, u32[]{:S(2)}) collective-permute-start(bf16[128,2048]{1,0:T(8,128)(2,1)} %collective-permute-done.17.rest_3_), channel_id=1, source_target_pairs={{0,1},{1,0},{2,3},{3,2},{4,5},{5,4},{6,7},{7,6},{8,9},{9,8},{10,11... | collective-permute-start | bytes 1572872 | tf_op jit(solution)/shard_map/ppermute | solution.py:490
  146.1 13.3 %collective-permute-start.23 = (bf16[128,2048]{1,0:T(8,128)(2,1)}, bf16[128,2048]{1,0:T(8,128)(2,1)}, u32[]{:S(2)}, u32[]{:S(2)}) collective-permute-start(bf16[128,2048]{1,0:T(8,128)(2,1)} %collective-permute-done.19.rest_5_), channel_id=1, source_target_pairs={{0,1},{1,0},{2,3},{3,2},{4,5},{5,4},{6,7},{7,6},{8,9},{9,8},{10,11... | collective-permute-start | bytes 1572872 | tf_op jit(solution)/shard_map/ppermute | solution.py:490
  (5 other events, 120.7 us)
